TPU v7x, 32 devices: a whole 2x2x4 slice. The times are simulated.
32 devices in a mesh: tm: 16 (over z, y, x), batch: 2 (over core).
Axes of the slice: x: 2, y: 2, z: 4, core: 2. Of those that a mesh axis runs over, the one named last changes fastest.
Arguments:
- state_map: float32 [512, 256, 256], P(('batch', 'tm')), parts along dimension 0, may hold values from -0.375 to 0.375
- input_map: float32 [512, 64, 256], P(('batch', 'tm')), parts along dimension 0, may hold values from -0.375 to 0.375
- closed_loop: float32 [512, 256, 256], P(('batch', 'tm')), parts along dimension 0, may hold values from -1.001 to 1.001
- feedback: float32 [512, 64, 256], P(('batch', 'tm')), parts along dimension 0, may hold values from -0.375 to 0.375
- value_matrix: float32 [512, 256, 256], P(('batch', 'tm')), parts along dimension 0, may hold values from -0.046875 to 1.5, as said below
- gain_inverse: float32 [512, 64, 64], P(('batch', 'tm')), parts along dimension 0, may hold values from -0.0105 to 0.2, as said below
- input_weight: float32 [128, 64], P('batch'), parts along dimension 0, may hold values from -0.36 to 6, as said below
- state_weight: float32 [512, 256], P(('batch', 'tm')), parts along dimension 0, may hold values from 0.1 to 3
- state_linear: float32 [512, 256], P(('batch', 'tm')), parts along dimension 0, may hold values from -0.18 to 0.18
- input_linear: float32 [512, 64], P(('batch', 'tm')), parts along dimension 0, may hold values from -0.18 to 0.18
- offset: float32 [512, 256], P(('batch', 'tm')), parts along dimension 0, may hold values from -0.18 to 0.18
- upper_bound: float32 [512, 64], P(('batch', 'tm')), parts along dimension 0, may hold values from 0.1 to 0.3
- states: float32 [512, 256], P(('batch', 'tm')), parts along dimension 0, may hold values from -0.18 to 0.18
- inputs: float32 [512, 64], P(('batch', 'tm')), parts along dimension 0, may hold values from -0.18 to 0.18
- multipliers: float32 [512, 256], P(('batch', 'tm')), parts along dimension 0, may hold values from -0.18 to 0.18
- bound_mult: float32 [512, 64], P(('batch', 'tm')), parts along dimension 0, may hold values from 0 to 0.06
- active: int32 [512, 64], P(('batch', 'tm')), parts along dimension 0, may hold values 0 or 1
Outputs:
- state_step: float32 [512, 256], P(('batch', 'tm')), parts along dimension 0
- input_step: float32 [512, 64], P(('batch', 'tm')), parts along dimension 0
- multiplier_step: float32 [512, 256], P(('batch', 'tm')), parts along dimension 0
- bound_step: float32 [512, 64], P(('batch', 'tm')), parts along dimension 0
- kkt_norms: float32 [6], P('batch'), parts along dimension 0
There are 2 independent parts, one for each index of `batch`. A program takes and returns all parts, laid end to end along the dimension named above; each array names one. Nothing has to cross between parts.
Inputs may be any that keep to these rules, and one draw needn't show every extreme that they name: `value_matrix`: each section's matrix is symmetric. `gain_inverse`: each section's matrix is symmetric. `input_weight`: symmetric.
All inputs are finite; a program needn't handle non-finite values. No bound on the sum of `active` on one device may be relied on, other than what follows from the above.
Results may differ from a plain program's by a relative error of at most 0.0003.
Values sent between devices are 32-bit elements; how exact they have to be, the bound alone decides.
A program may use at most 128 MiB of HBM per device.

v0:
```python
import functools
import jax
import jax.numpy as jnp
from jax import lax
from jax.experimental import pallas as pl
from jax.experimental.pallas import tpu as pltpu
from jax.sharding import PartitionSpec as P

F32 = jnp.float32
BF16 = jnp.bfloat16
PRECISE = lax.Precision.HIGHEST
MESH = pl.DeviceIdType.MESH
floor_share = 0.001
LANES = 128


def parts_of(x):
    high = x.astype(BF16)
    return high, (x - high.astype(F32)).astype(BF16)


def matmul(a, b):
    ah, al = parts_of(a)
    bh, bl = parts_of(b)
    dot = functools.partial(jnp.dot, preferred_element_type=F32)
    return dot(ah, bh) + (dot(ah, bl) + dot(al, bh))


def turned(x):
    rows, cols = x.shape
    up = -rows % LANES
    side = -cols % LANES
    if up:
        x = jnp.concatenate([x, jnp.zeros((up, cols), F32)], axis=0)
    if side:
        x = jnp.concatenate([x, jnp.zeros((rows + up, side), F32)], axis=1)
    return x.T[:cols, :rows]


def column(row):
    return jnp.broadcast_to(row, (LANES, row.shape[1])).T[:, :1]


def row_of(col):
    return jnp.broadcast_to(col, (col.shape[0], LANES)).T[:1]


def times(matrix, row):
    return jnp.sum(matrix * row, axis=1, keepdims=True)


def times_t(matrix, col):
    return jnp.sum(matrix * col, axis=0, keepdims=True)


def kernel(n, size, *refs):
    (a_hbm, b_hbm, m_hbm, k_hbm, v_hbm, gi_hbm, w_hbm, sw_hbm, sl_hbm, il_hbm, of_hbm, ub_hbm,
     st_hbm, in_hbm, mu_hbm, bm_hbm, ac_hbm,
     o_state, o_input, o_mult, o_bound, o_norm,
     a, b, m, fb, v, gi, w, sw, sl, il, of, ub, st, inp, mu, bm, ac,
     pre, suf, group, whole, sources, pushes, back_local, fwd_local, back,
     cols, fol_in, prd_in, prd_out, fol_out, vec_b, vec_f, ch_b_in, ch_f_in, ch_b_out, ch_f_out,
     load_sem, m_sem, nb_send, nb_recv, p_send, p_recv, b_send, b_recv, f_send, f_recv,
     ch_send, ch_recv) = refs
    me = lax.axis_index("tm")
    place = lax.rem(me, size)
    base = me - place
    at_group = lax.div(me, size)
    groups = n // size
    sections, ns = st.shape
    nu = inp.shape[1]
    half = sections // 2

    order = []
    for i in range(half):
        order += [i, sections - 1 - i]
    for k in order:
        pltpu.make_async_copy(m_hbm.at[k], m.at[k], m_sem.at[k]).start()
    small = [(w_hbm, w), (sw_hbm, sw), (sl_hbm, sl), (il_hbm, il), (of_hbm, of), (ub_hbm, ub),
             (st_hbm, st), (in_hbm, inp), (mu_hbm, mu), (bm_hbm, bm), (ac_hbm, ac)]
    large = [(a_hbm, a), (b_hbm, b), (v_hbm, v), (k_hbm, fb), (gi_hbm, gi)]
    loads = [
        pltpu.make_async_copy(src, dst, load_sem.at[i]) for i, (src, dst) in enumerate(small + large)
    ]
    for load in loads:
        load.start()

    barrier = pltpu.get_barrier_semaphore()
    first_of, last_of = place == 0, place == size - 1
    relations = [
        (jnp.logical_and(first_of, me > 0), me - 1),
        (jnp.logical_and(last_of, me < n - 1), me + 1),
        (at_group > 0, me - size),
        (at_group < groups - 1, me + size),
    ]
    mates = [base + lax.rem(place + j, size) for j in range(1, size)]
    for mate in mates:
        pl.semaphore_signal(barrier, inc=1, device_id={"tm": mate}, device_id_type=MESH)
    for holds, peer in relations:
        @pl.when(holds)
        def _():
            pl.semaphore_signal(barrier, inc=1, device_id={"tm": peer}, device_id_type=MESH)
    def remote(src, dst, send, recv, peer):
        return pltpu.make_async_remote_copy(
            src_ref=src, dst_ref=dst, send_sem=send, recv_sem=recv,
            device_id={"tm": peer}, device_id_type=MESH,
        )

    for load in loads[: len(small)]:
        load.wait()
    to_earlier = remote(fol_out, fol_in, nb_send.at[0], nb_recv.at[0], me - 1)
    to_later = remote(prd_out, prd_in, nb_send.at[1], nb_recv.at[1], me + 1)
    fol_out[...] = jnp.broadcast_to(mu[0:1], fol_out.shape)

    def wait_loop(k):
        pltpu.make_async_copy(m_hbm.at[k], m.at[k], m_sem.at[k]).wait()

    wait_loop(0)
    wait_loop(sections - 1)
    pre[0] = m[0]
    suf[sections - 1] = m[sections - 1]

    def grow(i, waits):
        j = sections - 1 - i
        if waits:
            wait_loop(i)
            wait_loop(j)
        pre[i] = matmul(m[i], pre[i - 1])
        suf[j] = matmul(suf[j + 1], m[j])

    @pl.loop(1, half)
    def _(i):
        grow(i, True)

    product = matmul(suf[half], pre[half - 1])
    suf[0] = product
    group[pl.ds(place, 1)] = product[None]
    peers = size - 1
    for holds, peer in relations:
        peers = peers + jnp.where(holds, 1, 0)
    pl.semaphore_wait(barrier, peers)

    @pl.when(me > 0)
    def _():
        to_earlier.start()

    along = place + 1 - 2 * lax.rem(place, 2)
    across = place + 2 - 4 * lax.div(place, 2)
    far = size - 1 - place
    top, bottom = pl.ds(0, ns // 2), pl.ds(ns // 2, ns // 2)

    def whole_block(slot, j, peer):
        return remote(group.at[slot], group.at[slot], p_send.at[j], p_recv.at[j], base + peer)

    def half_block(slot, rows, j, peer):
        ref = group.at[slot, rows]
        return remote(ref, ref, p_send.at[j], p_recv.at[j], base + peer)

    if size == 4:
        p_copies = [whole_block(place, 0, along), whole_block(place, 1, across)]
    else:
        p_copies = [
            whole_block(place, j, lax.rem(place + j + 1, size)) for j in range(size - 1)
        ]
    for copy in p_copies:
        copy.start()

    for load in loads[len(small):]:
        load.wait()
    lane = lax.broadcasted_iota(jnp.int32, (ns, LANES), 1)
    lane_u = lax.broadcasted_iota(jnp.int32, (nu, LANES), 1)

    inputs_t = turned(inp[...])
    acc = jnp.zeros((ns, LANES), F32)
    for k in range(sections):
        acc = jnp.where(lane == k, times(a[k], st[k:k + 1]), acc)
    predicted = acc.T[:sections]
    rows = [times_t(b[k], inputs_t[:, k:k + 1]) for k in range(sections)]
    predicted = predicted + jnp.concatenate(rows, axis=0)
    prd_out[...] = jnp.broadcast_to(predicted[sections - 1:], prd_out.shape)

    @pl.when(me < n - 1)
    def _():
        to_later.start()

    @pl.loop(half, sections - 1)
    def _(i):
        grow(i, False)

    @pl.when(me < n - 1)
    def _():
        to_earlier.wait_recv()

    @pl.when(me == n - 1)
    def _():
        fol_in[...] = jnp.zeros_like(fol_in)

    following = jnp.concatenate([mu[1:], fol_in[0:1]], axis=0)
    following_t = turned(following)
    grad_input = (
        jnp.dot(inp[...], w[...], precision=PRECISE, preferred_element_type=F32) + il[...] + bm[...]
    )
    acc = jnp.zeros((nu, LANES), F32)
    for k in range(sections):
        acc = jnp.where(lane_u == k, times(b[k], following[k:k + 1]), acc)
    grad_input = grad_input - turned(acc)[:sections]
    grad_input_t = turned(grad_input)
    rows = [times_t(a[k], following_t[:, k:k + 1]) for k in range(sections)]
    grad_state = sw[...] * st[...] + sl[...] + mu[...] - jnp.concatenate(rows, axis=0)

    @pl.when(me > 0)
    def _():
        to_later.wait_recv()

    @pl.when(me == 0)
    def _():
        prd_in[...] = jnp.zeros_like(prd_in)

    previous = jnp.concatenate([prd_in[0:1], predicted[:sections - 1]], axis=0)
    defect = st[...] - previous - of[...]
    defect_t = turned(defect)
    rows = [
        times_t(v[k], defect_t[:, k:k + 1]) + times_t(fb[k], grad_input_t[:, k:k + 1])
        for k in range(sections)
    ]
    sources[...] = jnp.concatenate(rows, axis=0) + grad_state
    slack = bm[...] * (ub[...] - inp[...])

    def total(*xs):
        return sum(
            jnp.sum(jnp.sum(x * x, axis=1, keepdims=True), axis=0, keepdims=True) for x in xs
        )

    sums = [total(defect), total(grad_state, grad_input), total(slack), total(of[...]),
            total(sl[...], il[...]), total(bm[...])]
    line = lax.broadcasted_iota(jnp.int32, (1, ns), 1)
    stats = jnp.zeros((1, ns), F32)
    for i, value in enumerate(sums):
        stats = jnp.where(line == i, value, stats)

    def packed(vector, extra):
        return jnp.concatenate([vector, extra, jnp.zeros((6, ns), F32)], axis=0)

    sources_t = turned(sources[...])
    costate = sources[0:1]
    for k in range(1, sections):
        costate = costate + times_t(pre[k - 1], sources_t[:, k:k + 1])
    vec_b[pl.ds(place, 1)] = packed(costate, stats)[None]
    b_copies = [
        remote(vec_b.at[place], vec_b.at[place], b_send.at[j], b_recv.at[j], mate)
        for j, mate in enumerate(mates)
    ]
    for copy in b_copies:
        copy.start()

    def arrive(buffer, send, recv):
        for j in range(size - 1):
            source = base + lax.rem(place + size - 1 - j, size)
            slot = source - base
            remote(buffer.at[slot], buffer.at[slot], send.at[j], recv.at[j], source).wait_recv()

    if size == 4:
        whole_block(along, 0, along).wait_recv()
        second = half_block(along, top, 2, across)
        second.start()
        whole_block(across, 1, across).wait_recv()
        third = half_block(across, bottom, 3, along)
        third.start()
        p_copies = p_copies + [second, third]

    costate = sources[sections - 1:]
    back_local[sections - 1:] = costate
    for k in range(sections - 2, -1, -1):
        costate = times_t(m[k], column(costate)) + sources[k:k + 1]
        back_local[k:k + 1] = costate

    arrive(vec_b, b_send, b_recv)
    if size == 4:
        half_block(far, top, 2, across).wait_recv()
        half_block(far, bottom, 3, along).wait_recv()
    else:
        arrive(group, p_send, p_recv)
    joined = group[0]
    for e in range(1, size):
        joined = matmul(group[e], joined)
    whole[...] = joined
    group_stats = jnp.sum(vec_b[:, 1, :], axis=0, keepdims=True)

    y = vec_b[size - 1, 0:1]
    for e in range(size - 2, -1, -1):
        y = vec_b[e, 0:1] + times_t(group[e], column(y))
    to_before = remote(ch_b_out, ch_b_in, ch_send.at[0], ch_recv.at[0], me - size)
    to_after = remote(ch_f_out, ch_f_in, ch_send.at[1], ch_recv.at[1], me + size)

    @pl.when(at_group < groups - 1)
    def _():
        to_before.wait_recv()

    @pl.when(at_group == groups - 1)
    def _():
        ch_b_in[...] = jnp.zeros_like(ch_b_in)

    incoming = ch_b_in[0:1]
    above = ch_b_in[1:2]
    ch_b_out[...] = packed(times_t(whole[...], column(incoming)) + y, above + group_stats)

    @pl.when(at_group > 0)
    def _():
        to_before.start()

    for e in range(size - 1, 0, -1):
        new = vec_b[e, 0:1] + times_t(group[e], column(incoming))
        incoming = jnp.where(place < e, new, incoming)

    incoming_c = column(incoming)
    for k in range(sections):
        back[k:k + 1] = times_t(suf[k], incoming_c) + back_local[k:k + 1]
    before = back[...]
    after = jnp.concatenate([before[1:], incoming], axis=0)
    acc = jnp.zeros((nu, LANES), F32)
    for k in range(sections):
        acc = jnp.where(lane_u == k, times(b[k], after[k:k + 1]), acc)
    pulled = turned(acc)[:sections]
    held = grad_input + pulled
    acc = jnp.zeros((nu, LANES), F32)
    for k in range(sections):
        gain = -times(gi[k], held[k:k + 1])
        acc = jnp.where(lane_u == k, gain, acc)
        pushes[k:k + 1] = times_t(b[k], gain)
    forward_gain = turned(acc)[:sections]

    acc = jnp.zeros((ns, ns), F32)
    for k in range(sections):
        drive = -defect[k:k + 1]
        if k:
            drive = drive + pushes[k - 1:k]
        acc = acc + suf[k] * drive
    ended = row_of(jnp.sum(acc, axis=1, keepdims=True)) + pushes[sections - 1:]
    vec_f[pl.ds(place, 1)] = packed(ended, stats)[None]
    f_copies = [
        remote(vec_f.at[place], vec_f.at[place], f_send.at[j], f_recv.at[j], mate)
        for j, mate in enumerate(mates)
    ]
    for copy in f_copies:
        copy.start()

    def forward_alone():
        step = -defect[0:1]
        acc = jnp.where(lane == 0, column(step), 0.0)
        for k in range(1, sections):
            moved = times(m[k - 1], step)
            step = row_of(moved) + pushes[k - 1:k] - defect[k:k + 1]
            acc = jnp.where(lane == k, column(step), acc)
        cols[...] = acc

    @pl.when(at_group > 0)
    def _():
        forward_alone()

    arrive(vec_f, f_send, f_recv)
    y = vec_f[0, 0:1]
    for e in range(1, size):
        y = vec_f[e, 0:1] + row_of(times(group[e], y))

    @pl.when(at_group > 0)
    def _():
        to_after.wait_recv()

    @pl.when(at_group == 0)
    def _():
        ch_f_in[...] = jnp.zeros_like(ch_f_in)

    entering = ch_f_in[0:1]
    below = ch_f_in[1:2]
    ch_f_out[...] = packed(row_of(times(whole[...], entering)) + y, below + group_stats)

    @pl.when(at_group < groups - 1)
    def _():
        to_after.start()

    @pl.when(at_group == 0)
    def _():
        forward_alone()

    for e in range(size - 1):
        new = vec_f[e, 0:1] + row_of(times(group[e], entering))
        entering = jnp.where(place > e, new, entering)

    acc = cols[...] + jnp.where(lane == 0, column(entering), 0.0)
    for k in range(1, sections):
        acc = acc + jnp.where(lane == k, times(pre[k - 1], entering), 0.0)
    state_step = acc.T[:sections]
    o_state[...] = state_step
    moved = acc[:, :sections] - defect_t
    for k in range(sections):
        o_mult[k:k + 1] = times_t(v[k], moved[:, k:k + 1]) + back[k:k + 1]
    acc = jnp.zeros((nu, LANES), F32)
    for k in range(sections):
        acc = jnp.where(lane_u == k, times(fb[k], state_step[k:k + 1]), acc)
    fed = turned(acc)[:sections]
    chosen = ac[...].astype(F32)
    input_step = (1.0 - chosen) * (fed + forward_gain) + chosen * (ub[...] - inp[...])
    o_input[...] = input_step
    o_bound[...] = chosen * (
        held + jnp.dot(input_step, w[...], precision=PRECISE, preferred_element_type=F32)
    )
    totals = above + group_stats + below
    tops = totals[:, 0:3]
    scale = totals[:, 3:6]
    spot = lax.broadcasted_iota(jnp.int32, (1, 3), 1)
    horizon = sections * n
    entries = jnp.where(spot == 0, ns, jnp.where(spot == 1, ns + nu, nu)).astype(F32)
    o_norm[...] = jnp.sqrt(tops / (scale + floor_share * horizon * entries))

    @pl.when(me > 0)
    def _():
        to_earlier.wait_send()

    @pl.when(me < n - 1)
    def _():
        to_later.wait_send()

    for copy in p_copies + b_copies + f_copies:
        copy.wait_send()

    @pl.when(at_group > 0)
    def _():
        to_before.wait_send()

    @pl.when(at_group < groups - 1)
    def _():
        to_after.wait_send()


def local(n, *args):
    size = 4 if n % 4 == 0 else (2 if n % 2 == 0 else 1)
    sections, ns = args[12].shape
    nu = args[13].shape[1]
    mates = size - 1
    copies = [pltpu.VMEM(x.shape, x.dtype) for x in args]
    message = (8, ns)
    dma = pltpu.SemaphoreType.DMA
    scratch = copies + [
        pltpu.VMEM((sections, ns, ns), F32),
        pltpu.VMEM((sections, ns, ns), F32),
        pltpu.VMEM((size, ns, ns), F32),
        pltpu.VMEM((ns, ns), F32),
        pltpu.VMEM((sections, ns), F32),
        pltpu.VMEM((sections, ns), F32),
        pltpu.VMEM((sections, ns), F32),
        pltpu.VMEM((sections, ns), F32),
        pltpu.VMEM((sections, ns), F32),
        pltpu.VMEM((ns, LANES), F32),
    ] + [pltpu.VMEM(message, F32)] * 4 + [
        pltpu.VMEM((size,) + message, F32),
        pltpu.VMEM((size,) + message, F32),
    ] + [pltpu.VMEM(message, F32)] * 4 + [
        dma((16,)), dma((sections,)), dma((2,)), dma((2,)),
        dma((4,)), dma((4,)), dma((mates,)), dma((mates,)), dma((mates,)), dma((mates,)),
        dma((2,)), dma((2,)),
    ]
    outs = [(sections, ns), (sections, nu), (sections, ns), (sections, nu), (1, 3)]
    results = pl.pallas_call(
        functools.partial(kernel, n, size),
        out_shape=[jax.ShapeDtypeStruct(shape, F32) for shape in outs],
        in_specs=[pl.BlockSpec(memory_space=pl.ANY)] * len(args),
        out_specs=[pl.BlockSpec(memory_space=pltpu.VMEM)] * len(outs),
        scratch_shapes=scratch,
        compiler_params=pltpu.CompilerParams(
            collective_id=0, has_side_effects=True, vmem_limit_bytes=60 * 1024 * 1024
        ),
    )(*args)
    return (*results[:4], results[4][0])


def solution(mesh):
    wide = P(("batch", "tm"), None, None)
    flat = P(("batch", "tm"), None)
    in_specs = (wide,) * 6 + (P("batch", None),) + (flat,) * 10
    out_specs = (flat,) * 4 + (P("batch"),)
    return jax.shard_map(
        functools.partial(local, mesh.shape["tm"]),
        mesh=mesh, in_specs=in_specs, out_specs=out_specs, check_vma=False,
    )
```

profile of v0, /device:TPU:24, one launch (start us, length us, event | category | flops | bytes accessed | tf_op | source)
XLA Modules:
  0.0 54.6 jit_solution(3735222342526450029)
XLA Ops:
  0.6 47.6 %shard_map.200 = (f32[16,256]{1,0:T(8,128)}, f32[16,64]{1,0:T(8,128)}, f32[16,256]{1,0:T(8,128)}, f32[16,64]{1,0:T(8,128)}, f32[1,3]{1,0:T(1,128)}) custom-call(f32[16,256,256]{2,1,0:T(8,128)} %refs_0_.1, f32[16,64,256]{2,1,0:T(8,128)} %refs_1_.1, f32[16,256,256]{2,1,0:T(8,128)} %refs_2_.1, f32[16,64,256]{2,1,0:T(8,128)} %refs_3_.1, ...), custom_call_target="tpu_custom_call" | custom-call | tf_op jit(solution)/shard_map/pallas_call | solution.py:463
  48.3 1.3 %copy.27 = f32[16,256]{1,0:T(8,128)} copy(f32[16,256]{1,0:T(8,128)} %get-tuple-element.20) | data formatting | bytes 32768
  49.6 1.3 %copy.28 = f32[16,64]{1,0:T(8,128)} copy(f32[16,64]{1,0:T(8,128)} %get-tuple-element.21) | data formatting | bytes 8192
  50.9 1.3 %copy.29 = f32[16,256]{1,0:T(8,128)} copy(f32[16,256]{1,0:T(8,128)} %get-tuple-element.22) | data formatting | bytes 32768
  52.2 1.3 %copy.30 = f32[16,64]{1,0:T(8,128)} copy(f32[16,64]{1,0:T(8,128)} %get-tuple-element.23) | data formatting | bytes 8192
  53.5 1.1 %copy.31 = f32[3]{0:T(128)} copy(f32[3]{0:T(128)} %bitcast.1) | data formatting | bytes 24
where the time goes:
time: 55.1 us; the launch traced here: 54.6 us
  Pallas kernels  47.6 us (86%)
  local copies, waits for them, and re-layouts  6.35 us (12%)
  between operations  0.65 us (1%)
    pallas_call x1, Pallas kernels, local(): pl.pallas_call(functools.partial(kernel, n, size), out_shape=[jax.ShapeDt...  47.6 us
    unnamed x5, local copies, waits for them, and re-layouts  6.35 us

commit v1 on v0

--- a/solution.py
+++ b/solution.py
@@ -12,6 +12,7 @@
 MESH = pl.DeviceIdType.MESH
 floor_share = 0.001
 LANES = 128
+VMEM_LIMIT = 48 * 1024 * 1024
 
 
 def parts_of(x):
@@ -56,7 +57,7 @@
 def kernel(n, size, *refs):
     (a_hbm, b_hbm, m_hbm, k_hbm, v_hbm, gi_hbm, w_hbm, sw_hbm, sl_hbm, il_hbm, of_hbm, ub_hbm,
      st_hbm, in_hbm, mu_hbm, bm_hbm, ac_hbm,
-     o_state, o_input, o_mult, o_bound, o_norm,
+     packed_out,
      a, b, m, fb, v, gi, w, sw, sl, il, of, ub, st, inp, mu, bm, ac,
      pre, suf, group, whole, sources, pushes, back_local, fwd_local, back,
      cols, fol_in, prd_in, prd_out, fol_out, vec_b, vec_f, ch_b_in, ch_f_in, ch_b_out, ch_f_out,
@@ -390,19 +391,21 @@
     for k in range(1, sections):
         acc = acc + jnp.where(lane == k, times(pre[k - 1], entering), 0.0)
     state_step = acc.T[:sections]
-    o_state[...] = state_step
+    packed_out[0:sections] = state_step
     moved = acc[:, :sections] - defect_t
     for k in range(sections):
-        o_mult[k:k + 1] = times_t(v[k], moved[:, k:k + 1]) + back[k:k + 1]
+        packed_out[sections + k:sections + k + 1] = times_t(v[k], moved[:, k:k + 1]) + back[k:k + 1]
     acc = jnp.zeros((nu, LANES), F32)
     for k in range(sections):
         acc = jnp.where(lane_u == k, times(fb[k], state_step[k:k + 1]), acc)
     fed = turned(acc)[:sections]
     chosen = ac[...].astype(F32)
     input_step = (1.0 - chosen) * (fed + forward_gain) + chosen * (ub[...] - inp[...])
-    o_input[...] = input_step
-    o_bound[...] = chosen * (
+    bound_step = chosen * (
         held + jnp.dot(input_step, w[...], precision=PRECISE, preferred_element_type=F32)
+    )
+    packed_out[2 * sections:3 * sections] = jnp.concatenate(
+        [input_step, bound_step, jnp.zeros((sections, ns - 2 * nu), F32)], axis=1
     )
     totals = above + group_stats + below
     tops = totals[:, 0:3]
@@ -410,7 +413,8 @@
     spot = lax.broadcasted_iota(jnp.int32, (1, 3), 1)
     horizon = sections * n
     entries = jnp.where(spot == 0, ns, jnp.where(spot == 1, ns + nu, nu)).astype(F32)
-    o_norm[...] = jnp.sqrt(tops / (scale + floor_share * horizon * entries))
+    norms = jnp.sqrt(tops / (scale + floor_share * horizon * entries))
+    packed_out[3 * sections:3 * sections + 1, 0:3] = norms
 
     @pl.when(me > 0)
     def _():
@@ -430,6 +434,14 @@
     @pl.when(at_group < groups - 1)
     def _():
         to_after.wait_send()
+
+
+def spread(sections, ns, nu, packed, o_state, o_input, o_mult, o_bound, o_norm):
+    o_state[...] = packed[0:sections]
+    o_mult[...] = packed[sections:2 * sections]
+    o_input[...] = packed[2 * sections:3 * sections, 0:nu]
+    o_bound[...] = packed[2 * sections:3 * sections, nu:2 * nu]
+    o_norm[...] = packed[3 * sections:3 * sections + 1, 0:3]
 
 
 def local(n, *args):
@@ -459,17 +471,25 @@
         dma((4,)), dma((4,)), dma((mates,)), dma((mates,)), dma((mates,)), dma((mates,)),
         dma((2,)), dma((2,)),
     ]
+    args = [pltpu.with_memory_space_constraint(x, pltpu.HBM) for x in args]
+    packed = pl.pallas_call(
+        functools.partial(kernel, n, size),
+        out_shape=jax.ShapeDtypeStruct((3 * sections + 8, ns), F32),
+        in_specs=[pl.BlockSpec(memory_space=pltpu.HBM)] * len(args),
+        out_specs=pl.BlockSpec(memory_space=pltpu.VMEM),
+        scratch_shapes=scratch,
+        compiler_params=pltpu.CompilerParams(
+            collective_id=0, has_side_effects=True, vmem_limit_bytes=VMEM_LIMIT
+        ),
+    )(*args)
     outs = [(sections, ns), (sections, nu), (sections, ns), (sections, nu), (1, 3)]
     results = pl.pallas_call(
-        functools.partial(kernel, n, size),
+        functools.partial(spread, sections, ns, nu),
         out_shape=[jax.ShapeDtypeStruct(shape, F32) for shape in outs],
-        in_specs=[pl.BlockSpec(memory_space=pl.ANY)] * len(args),
+        in_specs=[pl.BlockSpec(memory_space=pltpu.VMEM)],
         out_specs=[pl.BlockSpec(memory_space=pltpu.VMEM)] * len(outs),
-        scratch_shapes=scratch,
-        compiler_params=pltpu.CompilerParams(
-            collective_id=0, has_side_effects=True, vmem_limit_bytes=60 * 1024 * 1024
-        ),
-    )(*args)
+        compiler_params=pltpu.CompilerParams(vmem_limit_bytes=4 * 1024 * 1024),
+    )(packed)
     return (*results[:4], results[4][0])
 
 

time: 55.1 us -> 48.8 us (0.89)
  local copies, waits for them, and re-layouts: 6.35 us -> 0 us
    unnamed x5 -> x0, local copies, waits for them, and re-layouts: 6.35 us -> none
    pallas_call x1 -> x2, Pallas kernels: 47.6 us -> 48 us  [the longest x1 47.3 us: local(): pl.pallas_call(functools.partial(kernel, n, size), out_shape=jax.ShapeDty...]
where the time goes in v1:
time: 48.8 us; the launch traced here: 48.6 us
  Pallas kernels  48 us (98%)
  between operations  0.65 us (1%)
    pallas_call x1, Pallas kernels, local(): pl.pallas_call(functools.partial(kernel, n, size), out_shape=jax.ShapeDty...  47.3 us

profile of v1, /device:TPU:24, one launch (start us, length us, event | category | flops | bytes accessed | tf_op | source)
XLA Modules:
  0.0 48.6 jit_solution(8850069956415412992)
XLA Ops:
  0.6 47.3 %shard_map.200.packed = f32[56,256]{1,0:T(8,128)S(1)} custom-call(f32[16,256,256]{2,1,0:T(8,128)} %refs_0_.1, f32[16,64,256]{2,1,0:T(8,128)} %refs_1_.1, f32[16,256,256]{2,1,0:T(8,128)} %refs_2_.1, f32[16,64,256]{2,1,0:T(8,128)} %refs_3_.1, f32[16,256,256]{2,1,0:T(8,128)} %refs_4_.1, f32[16,64,64]{2,1,0:T(8,128)} %refs_5_.1, f32[64,64]{1,0:T(8,128)} %refs_6_.1, ...), custom_call_target="tpu_custom_call" | custom-call | tf_op jit(solution)/shard_map/pallas_call | solution.py:475
  47.9 0.7 %shard_map.201 = (f32[16,256]{1,0:T(8,128)}, f32[16,64]{1,0:T(8,128)}, f32[16,256]{1,0:T(8,128)}, f32[16,64]{1,0:T(8,128)}, f32[1,3]{1,0:T(1,128)}) custom-call(f32[56,256]{1,0:T(8,128)S(1)} %shard_map.200.packed), custom_call_target="tpu_custom_call" | custom-call | tf_op jit(solution)/shard_map/pallas_call | solution.py:486

commit v2 on v1

v2 whole, which is shorter than its diff:
```python
import functools
import jax
import jax.numpy as jnp
from jax import lax
from jax.experimental import pallas as pl
from jax.experimental.pallas import tpu as pltpu
from jax.sharding import PartitionSpec as P

F32 = jnp.float32
BF16 = jnp.bfloat16
PRECISE = lax.Precision.HIGHEST
MESH = pl.DeviceIdType.MESH
floor_share = 0.001
LANES = 128
VMEM_LIMIT = 48 * 1024 * 1024


def parts_of(x):
    high = x.astype(BF16)
    return high, (x - high.astype(F32)).astype(BF16)


def matmul(a, b):
    ah, al = parts_of(a)
    bh, bl = parts_of(b)
    dot = functools.partial(jnp.dot, preferred_element_type=F32)
    return dot(ah, bh) + (dot(ah, bl) + dot(al, bh))


def turned(x):
    rows, cols = x.shape
    up = -rows % LANES
    side = -cols % LANES
    if up:
        x = jnp.concatenate([x, jnp.zeros((up, cols), F32)], axis=0)
    if side:
        x = jnp.concatenate([x, jnp.zeros((rows + up, side), F32)], axis=1)
    return x.T[:cols, :rows]


def column(row):
    return jnp.broadcast_to(row, (LANES, row.shape[1])).T[:, :1]


def row_of(col):
    return jnp.broadcast_to(col, (col.shape[0], LANES)).T[:1]


def times(matrix, row):
    return jnp.sum(matrix * row, axis=1, keepdims=True)


def times_t(matrix, col):
    return jnp.sum(matrix * col, axis=0, keepdims=True)


def column_block(row):
    return jnp.broadcast_to(row, (LANES, row.shape[1])).T


def lift(matrix, block):
    cols = matrix.shape[1]
    parts = [
        jnp.sum(matrix[:, j:j + LANES] * block[:, :min(LANES, cols - j)], axis=0, keepdims=True)
        for j in range(0, cols, LANES)
    ]
    return jnp.concatenate(parts, axis=1) if len(parts) > 1 else parts[0]


def kernel(n, size, *refs):
    (a_hbm, b_hbm, m_hbm, k_hbm, v_hbm, gi_hbm, w_hbm, sw_hbm, sl_hbm, il_hbm, of_hbm, ub_hbm,
     st_hbm, in_hbm, mu_hbm, bm_hbm, ac_hbm,
     packed_out,
     a, b, m, fb, v, gi, w, sw, sl, il, of, ub, st, inp, mu, bm, ac,
     pre, suf, group, heads, tails, turned_w, turned_r,
     sources, pushes, back_local, back, cols,
     fol_in, prd_in, prd_out, fol_out, vec_b, vec_f, direct_in, direct_out,
     ch_b_in, ch_f_in, ch_b_out, ch_f_out,
     load_sem, m_sem, nb_send, nb_recv, p_send, p_recv, b_send, b_recv, f_send, f_recv,
     d_send, d_recv, ch_send, ch_recv) = refs
    me = lax.axis_index("tm")
    place = lax.rem(me, size)
    base = me - place
    at_group = lax.div(me, size)
    groups = n // size
    sections, ns = st.shape
    nu = inp.shape[1]
    half = sections // 2
    last = sections - 1
    first_group, top_group = at_group == 0, at_group == groups - 1

    early = [(st_hbm, st), (in_hbm, inp), (mu_hbm, mu),
             (a_hbm.at[last], a.at[last]), (b_hbm.at[last], b.at[last])]
    small = [(w_hbm, w), (sw_hbm, sw), (sl_hbm, sl), (il_hbm, il), (of_hbm, of), (ub_hbm, ub),
             (bm_hbm, bm), (ac_hbm, ac)]
    rest = pl.ds(0, last)
    large = [(a_hbm.at[rest], a.at[rest]), (b_hbm.at[rest], b.at[rest]), (v_hbm, v), (k_hbm, fb),
             (gi_hbm, gi)]
    loads = [
        pltpu.make_async_copy(src, dst, load_sem.at[i])
        for i, (src, dst) in enumerate(early + small + large)
    ]
    m_loads = [pltpu.make_async_copy(m_hbm.at[k], m.at[k], m_sem.at[k]) for k in range(sections)]
    for i in range(half):
        m_loads[i].start()
        m_loads[half + i].start()
    for load in loads[:len(early)]:
        load.start()

    barrier = pltpu.get_barrier_semaphore()
    mates = [base + lax.rem(place + j, size) for j in range(1, size)]

    def greet(peer):
        pl.semaphore_signal(barrier, inc=1, device_id={"tm": peer}, device_id_type=MESH)

    for mate in mates:
        greet(mate)
    for has, start in ((jnp.logical_not(first_group), base - size),
                       (jnp.logical_not(top_group), base + size)):
        @pl.when(has)
        def _():
            for j in range(size):
                greet(start + j)

    def remote(src, dst, send, recv, peer):
        return pltpu.make_async_remote_copy(
            src_ref=src, dst_ref=dst, send_sem=send, recv_sem=recv,
            device_id={"tm": peer}, device_id_type=MESH,
        )

    for load in loads[:len(early)]:
        load.wait()
    m_loads[0].wait()
    m_loads[half].wait()
    for load in loads[len(early):]:
        load.start()
    for k in range(1, half):
        m_loads[k].wait()
        m_loads[half + k].wait()

    fol_out[...] = mu[0:1]
    moved = row_of(times(a[last], st[last:]))
    prd_out[...] = moved + lift(b[last], column_block(
        jnp.concatenate([inp[last:], jnp.zeros((1, LANES - nu), F32)], axis=1))[:nu])

    lines = [[m.at[k] for k in range(half)], [m.at[k] for k in range(half, sections)]]
    temps = [[suf.at[i] for i in range(half)], [pre.at[half + i] for i in range(half)]]
    ends = [pre.at[half - 1], suf.at[half]]
    while len(lines[0]) > 1:
        grown = [[], []]
        for i in range(0, len(lines[0]) - 1, 2):
            for side, line in enumerate(lines):
                dst = ends[side] if len(line) == 2 else temps[side].pop(0)
                dst[...] = matmul(line[i + 1][...], line[i][...])
                grown[side].append(dst)
        if len(lines[0]) % 2:
            for side, line in enumerate(lines):
                grown[side].append(line[-1])
        lines = grown

    peers = size - 1 + jnp.where(first_group, 0, size) + jnp.where(top_group, 0, size)
    pl.semaphore_wait(barrier, peers)
    to_earlier = remote(fol_out, fol_in, nb_send.at[0], nb_recv.at[0], me - 1)
    to_later = remote(prd_out, prd_in, nb_send.at[1], nb_recv.at[1], me + 1)

    @pl.when(me > 0)
    def _():
        to_earlier.start()

    @pl.when(me < n - 1)
    def _():
        to_later.start()

    along = place + 1 - 2 * lax.rem(place, 2)
    across = place + 2 - 4 * lax.div(place, 2)
    far = size - 1 - place
    top, bottom = pl.ds(0, ns // 2), pl.ds(ns // 2, ns // 2)

    def piece(slot, rows, j, peer):
        ref = group.at[slot, rows]
        return remote(ref, ref, p_send.at[j], p_recv.at[j], base + peer)

    product = matmul(suf[half], pre[half - 1])
    group[pl.ds(place, 1)] = product[None]
    if size == 4:
        p_copies = [piece(place, top, 0, along), piece(place, bottom, 2, across),
                    piece(place, bottom, 1, along), piece(place, top, 3, across)]
    else:
        p_copies = [
            remote(group.at[place], group.at[place], p_send.at[j], p_recv.at[j],
                   base + lax.rem(place + j + 1, size))
            for j in range(size - 1)
        ]
    for copy in p_copies:
        copy.start()
    suf[0] = product

    pre[0] = m[0]
    suf[last] = m[last]
    pre[half] = matmul(m[half], pre[half - 1])
    suf[half - 1] = matmul(suf[half], m[half - 1])

    def grow(i):
        pre[half + i] = matmul(m[half + i], pre[half + i - 1])
        suf[half - 1 - i] = matmul(suf[half - i], m[half - 1 - i])
        pre[i] = matmul(m[i], pre[i - 1])
        suf[last - i] = matmul(suf[sections - i], m[last - i])

    split = half // 2

    @pl.loop(1, split)
    def _(i):
        grow(i)

    for load in loads[len(early):]:
        load.wait()
    lane = lax.broadcasted_iota(jnp.int32, (ns, LANES), 1)
    lane_u = lax.broadcasted_iota(jnp.int32, (nu, LANES), 1)

    inputs_t = turned(inp[...])
    acc = jnp.zeros((ns, LANES), F32)
    for k in range(sections):
        acc = jnp.where(lane == k, times(a[k], st[k:k + 1]), acc)
    predicted = acc.T[:sections]
    rows = [times_t(b[k], inputs_t[:, k:k + 1]) for k in range(sections)]
    predicted = predicted + jnp.concatenate(rows, axis=0)

    @pl.when(me < n - 1)
    def _():
        to_earlier.wait_recv()

    @pl.when(me == n - 1)
    def _():
        fol_in[...] = jnp.zeros_like(fol_in)

    following = jnp.concatenate([mu[1:], fol_in[...]], axis=0)
    following_t = turned(following)
    grad_input = (
        jnp.dot(inp[...], w[...], precision=PRECISE, preferred_element_type=F32) + il[...] + bm[...]
    )
    acc = jnp.zeros((nu, LANES), F32)
    for k in range(sections):
        acc = jnp.where(lane_u == k, times(b[k], following[k:k + 1]), acc)
    grad_input = grad_input - turned(acc)[:sections]
    grad_input_t = turned(grad_input)
    rows = [times_t(a[k], following_t[:, k:k + 1]) for k in range(sections)]
    grad_state = sw[...] * st[...] + sl[...] + mu[...] - jnp.concatenate(rows, axis=0)

    @pl.when(me > 0)
    def _():
        to_later.wait_recv()

    @pl.when(me == 0)
    def _():
        prd_in[...] = jnp.zeros_like(prd_in)

    previous = jnp.concatenate([prd_in[...], predicted[:last]], axis=0)
    defect = st[...] - previous - of[...]
    defect_t = turned(defect)
    rows = [
        times_t(v[k], defect_t[:, k:k + 1]) + times_t(fb[k], grad_input_t[:, k:k + 1])
        for k in range(sections)
    ]
    sources[...] = jnp.concatenate(rows, axis=0) + grad_state
    slack = bm[...] * (ub[...] - inp[...])

    if size == 4:
        piece(along, top, 0, along).wait_recv()
        relays = [piece(along, top, 4, across), piece(across, bottom, 5, along)]
        relays[0].start()
        piece(across, bottom, 2, across).wait_recv()
        relays[1].start()
        p_copies = p_copies + relays

    def total(*xs):
        return sum(
            jnp.sum(jnp.sum(x * x, axis=1, keepdims=True), axis=0, keepdims=True) for x in xs
        )

    sums = [total(defect), total(grad_state, grad_input), total(slack), total(of[...]),
            total(sl[...], il[...]), total(bm[...])]
    line = lax.broadcasted_iota(jnp.int32, (1, ns), 1)
    stats = jnp.zeros((1, ns), F32)
    for i, value in enumerate(sums):
        stats = jnp.where(line == i, value, stats)

    def packed(vector, extra):
        return jnp.concatenate([vector, extra], axis=0)

    costate = sources[last:]
    back_local[last:] = costate
    for k in range(last - 1, -1, -1):
        costate = lift(m[k], column_block(costate)) + sources[k:k + 1]
        back_local[k:k + 1] = costate
    vec_b[pl.ds(place, 1)] = packed(costate, stats)[None]
    b_copies = [
        remote(vec_b.at[place], vec_b.at[place], b_send.at[j], b_recv.at[j], mate)
        for j, mate in enumerate(mates)
    ]
    for copy in b_copies:
        copy.start()

    @pl.loop(split, half - 1)
    def _(i):
        grow(i)

    def arrive(buffer, send, recv):
        for j in range(size - 1):
            source = base + lax.rem(place + size - 1 - j, size)
            slot = source - base
            remote(buffer.at[slot], buffer.at[slot], send.at[j], recv.at[j], source).wait_recv()

    arrive(vec_b, b_send, b_recv)
    if size == 4:
        piece(along, bottom, 1, along).wait_recv()
        piece(across, top, 3, across).wait_recv()
        piece(far, top, 4, across).wait_recv()
        piece(far, bottom, 5, along).wait_recv()
    else:
        arrive(group, p_send, p_recv)
    group_stats = jnp.sum(vec_b[:, 1, :], axis=0, keepdims=True)

    held_in = jnp.zeros((1, ns), F32)
    y = vec_b[size - 1, 0:1]
    for e in range(size - 2, -1, -1):
        held_in = jnp.where(place == e, y, held_in)
        y = vec_b[e, 0:1] + lift(group[e], column_block(y))
    to_before = remote(ch_b_out, ch_b_in, ch_send.at[0], ch_recv.at[0], me - size)
    to_after = remote(ch_f_out, ch_f_in, ch_send.at[1], ch_recv.at[1], me + size)

    @pl.when(top_group)
    def _():
        ch_b_in[...] = jnp.zeros_like(ch_b_in)
        ch_b_out[...] = packed(y, group_stats)

    @pl.when(jnp.logical_and(top_group, jnp.logical_not(first_group)))
    def _():
        to_before.start()

    unit = (lax.broadcasted_iota(jnp.int32, (ns, ns), 0)
            == lax.broadcasted_iota(jnp.int32, (ns, ns), 1)).astype(F32)
    heads[0] = unit
    tails[size - 1] = unit
    for e in range(1, size):
        heads[e] = group[0] if e == 1 else matmul(group[e - 1], heads[e - 1])
        f = size - 1 - e
        tails[f] = group[size - 1] if e == 1 else matmul(tails[f + 1], group[f + 1])
    whole = matmul(group[size - 1], heads[size - 1]) if size > 1 else group[0]
    heads[size] = whole

    for k in range(1, last, 2):
        m[k] = m[k].T

    @pl.when(jnp.logical_not(top_group))
    def _():
        to_before.wait_recv()
        ch_b_out[...] = packed(
            y + lift(heads[size], column_block(ch_b_in[0:1])), ch_b_in[1:2] + group_stats
        )

    @pl.when(jnp.logical_not(jnp.logical_or(top_group, first_group)))
    def _():
        to_before.start()

    above = ch_b_in[1:2]
    incoming = held_in + lift(tails[place], column_block(ch_b_in[0:1]))
    incoming_c = column_block(incoming)
    for k in range(sections):
        back[k:k + 1] = lift(suf[k], incoming_c) + back_local[k:k + 1]
    before = back[...]
    after = jnp.concatenate([before[1:], incoming], axis=0)
    acc = jnp.zeros((nu, LANES), F32)
    for k in range(sections):
        acc = jnp.where(lane_u == k, times(b[k], after[k:k + 1]), acc)
    pulled = turned(acc)[:sections]
    held = grad_input + pulled
    acc = jnp.zeros((nu, LANES), F32)
    for k in range(sections):
        gain = -times(gi[k], held[k:k + 1])
        acc = jnp.where(lane_u == k, gain, acc)
        pushes[k:k + 1] = times_t(b[k], gain)
    forward_gain = turned(acc)[:sections]

    acc = jnp.zeros((ns, ns), F32)
    for k in range(sections):
        drive = -defect[k:k + 1]
        if k:
            drive = drive + pushes[k - 1:k]
        acc = acc + suf[k] * drive
    ended = row_of(jnp.sum(acc, axis=1, keepdims=True)) + pushes[last:]
    vec_f[pl.ds(place, 1)] = ended[None]
    f_copies = [
        remote(vec_f.at[place], vec_f.at[place], f_send.at[j], f_recv.at[j], mate)
        for j, mate in enumerate(mates)
    ]
    direct = [
        remote(direct_out, direct_in.at[place], d_send.at[j], d_recv.at[place], base + size + j)
        for j in range(size)
    ]
    sends_direct = jnp.logical_and(first_group, jnp.logical_not(top_group))

    @pl.when(sends_direct)
    def _():
        direct_out[...] = packed(row_of(times(tails[place], ended)), group_stats)
        for copy in direct:
            copy.start()

    for copy in f_copies:
        copy.start()
    turned_w[...] = heads[size].T
    turned_r[...] = heads[place].T

    drive = jnp.concatenate([jnp.zeros((1, ns), F32), pushes[:last]], axis=0) - defect
    drive_t = turned(drive)
    step = drive[0:1]
    kept = [step]
    acc = jnp.zeros((ns, LANES), F32)
    for k in range(1, sections):
        if k % 2:
            block = jnp.broadcast_to(times(m[k - 1], step), (ns, LANES)) + drive_t[:, k:k + 1]
            acc = jnp.where(lane == k, block, acc)
            kept.append(jnp.zeros((1, ns), F32))
        else:
            step = lift(m[k - 1], block) + drive[k:k + 1]
            kept.append(step)
    kept.append(jnp.zeros((LANES - sections, ns), F32))
    cols[...] = acc + jnp.concatenate(kept, axis=0).T

    arrive(vec_f, f_send, f_recv)
    held_on = jnp.zeros((1, ns), F32)
    y = vec_f[0]
    for e in range(1, size):
        held_on = jnp.where(place == e, y, held_on)
        y = vec_f[e] + row_of(times(group[e], y))

    @pl.when(first_group)
    def _():
        ch_f_in[...] = jnp.zeros_like(ch_f_in)

    @pl.when(at_group == 1)
    def _():
        came = jnp.zeros((1, ns), F32)
        for j in range(size):
            remote(direct_out, direct_in.at[j], d_send.at[j], d_recv.at[j],
                   base - size + j).wait_recv()
            came = came + direct_in[j, 0:1]
        ch_f_in[...] = packed(came, direct_in[0, 1:2])

    @pl.when(at_group > 1)
    def _():
        to_after.wait_recv()

    below = ch_f_in[1:2]
    entering_c = column_block(ch_f_in[0:1])
    goes_on = jnp.logical_and(jnp.logical_not(first_group), jnp.logical_not(top_group))

    @pl.when(goes_on)
    def _():
        ch_f_out[...] = packed(y + lift(turned_w[...], entering_c), below + group_stats)
        to_after.start()

    entering = held_on + lift(turned_r[...], entering_c)

    acc = cols[...] + jnp.where(lane == 0, column(entering), 0.0)
    for k in range(1, sections):
        acc = acc + jnp.where(lane == k, times(pre[k - 1], entering), 0.0)
    state_step = acc.T[:sections]
    packed_out[0:sections] = state_step
    moved = acc[:, :sections] - defect_t
    for k in range(sections):
        packed_out[sections + k:sections + k + 1] = times_t(v[k], moved[:, k:k + 1]) + back[k:k + 1]
    acc = jnp.zeros((nu, LANES), F32)
    for k in range(sections):
        acc = jnp.where(lane_u == k, times(fb[k], state_step[k:k + 1]), acc)
    fed = turned(acc)[:sections]
    chosen = ac[...].astype(F32)
    input_step = (1.0 - chosen) * (fed + forward_gain) + chosen * (ub[...] - inp[...])
    bound_step = chosen * (
        held + jnp.dot(input_step, w[...], precision=PRECISE, preferred_element_type=F32)
    )
    packed_out[2 * sections:3 * sections] = jnp.concatenate(
        [input_step, bound_step, jnp.zeros((sections, ns - 2 * nu), F32)], axis=1
    )
    totals = above + group_stats + below
    tops = totals[:, 0:3]
    scale = totals[:, 3:6]
    spot = lax.broadcasted_iota(jnp.int32, (1, 3), 1)
    horizon = sections * n
    entries = jnp.where(spot == 0, ns, jnp.where(spot == 1, ns + nu, nu)).astype(F32)
    norms = jnp.sqrt(tops / (scale + floor_share * horizon * entries))
    packed_out[3 * sections:3 * sections + 1, 0:3] = norms

    @pl.when(me > 0)
    def _():
        to_earlier.wait_send()

    @pl.when(me < n - 1)
    def _():
        to_later.wait_send()

    for copy in p_copies + b_copies + f_copies:
        copy.wait_send()

    @pl.when(jnp.logical_not(first_group))
    def _():
        to_before.wait_send()

    @pl.when(sends_direct)
    def _():
        for copy in direct:
            copy.wait_send()

    @pl.when(goes_on)
    def _():
        to_after.wait_send()


def spread(sections, ns, nu, packed, o_state, o_input, o_mult, o_bound, o_norm):
    o_state[...] = packed[0:sections]
    o_mult[...] = packed[sections:2 * sections]
    o_input[...] = packed[2 * sections:3 * sections, 0:nu]
    o_bound[...] = packed[2 * sections:3 * sections, nu:2 * nu]
    o_norm[...] = packed[3 * sections:3 * sections + 1, 0:3]


def local(n, *args):
    size = 4 if n % 4 == 0 else (2 if n % 2 == 0 else 1)
    sections, ns = args[12].shape
    nu = args[13].shape[1]
    mates = size - 1
    copies = [pltpu.VMEM(x.shape, x.dtype) for x in args]
    dma = pltpu.SemaphoreType.DMA
    scratch = copies + [
        pltpu.VMEM((sections, ns, ns), F32),
        pltpu.VMEM((sections, ns, ns), F32),
        pltpu.VMEM((size, ns, ns), F32),
        pltpu.VMEM((size + 1, ns, ns), F32),
        pltpu.VMEM((size, ns, ns), F32),
        pltpu.VMEM((ns, ns), F32),
        pltpu.VMEM((ns, ns), F32),
        pltpu.VMEM((sections, ns), F32),
        pltpu.VMEM((sections, ns), F32),
        pltpu.VMEM((sections, ns), F32),
        pltpu.VMEM((sections, ns), F32),
        pltpu.VMEM((ns, LANES), F32),
    ] + [pltpu.VMEM((1, ns), F32)] * 4 + [
        pltpu.VMEM((size, 2, ns), F32),
        pltpu.VMEM((size, 1, ns), F32),
        pltpu.VMEM((size, 2, ns), F32),
    ] + [pltpu.VMEM((2, ns), F32)] * 5 + [
        dma((18,)), dma((sections,)), dma((2,)), dma((2,)),
        dma((6,)), dma((6,)), dma((mates,)), dma((mates,)), dma((mates,)), dma((mates,)),
        dma((size,)), dma((size,)), dma((2,)), dma((2,)),
    ]
    args = [pltpu.with_memory_space_constraint(x, pltpu.HBM) for x in args]
    packed = pl.pallas_call(
        functools.partial(kernel, n, size),
        out_shape=jax.ShapeDtypeStruct((3 * sections + 8, ns), F32),
        in_specs=[pl.BlockSpec(memory_space=pltpu.HBM)] * len(args),
        out_specs=pl.BlockSpec(memory_space=pltpu.VMEM),
        scratch_shapes=scratch,
        compiler_params=pltpu.CompilerParams(
            collective_id=0, has_side_effects=True, vmem_limit_bytes=VMEM_LIMIT
        ),
    )(*args)
    outs = [(sections, ns), (sections, nu), (sections, ns), (sections, nu), (1, 3)]
    results = pl.pallas_call(
        functools.partial(spread, sections, ns, nu),
        out_shape=[jax.ShapeDtypeStruct(shape, F32) for shape in outs],
        in_specs=[pl.BlockSpec(memory_space=pltpu.VMEM)],
        out_specs=[pl.BlockSpec(memory_space=pltpu.VMEM)] * len(outs),
        compiler_params=pltpu.CompilerParams(vmem_limit_bytes=4 * 1024 * 1024),
    )(packed)
    return (*results[:4], results[4][0])


def solution(mesh):
    wide = P(("batch", "tm"), None, None)
    flat = P(("batch", "tm"), None)
    in_specs = (wide,) * 6 + (P("batch", None),) + (flat,) * 10
    out_specs = (flat,) * 4 + (P("batch"),)
    return jax.shard_map(
        functools.partial(local, mesh.shape["tm"]),
        mesh=mesh, in_specs=in_specs, out_specs=out_specs, check_vma=False,
    )
```

time: 48.8 us -> 38.6 us (0.79)
  Pallas kernels: 48 us -> 37.8 us
    pallas_call x1, Pallas kernels: 47.3 us -> 37.2 us  [local(): pl.pallas_call(functools.partial(kernel, n, size), out_shape=jax.ShapeDty...]
where the time goes in v2:
time: 38.6 us; the launch traced here: 38.5 us
  Pallas kernels  37.8 us (98%)
  between operations  0.65 us (2%)
    pallas_call x1, Pallas kernels, local(): pl.pallas_call(functools.partial(kernel, n, size), out_shape=jax.ShapeDty...  37.2 us

profile of v2, /device:TPU:24, one launch (start us, length us, event | category | flops | bytes accessed | tf_op | source)
XLA Modules:
  0.0 38.5 jit_solution(13063213785318326067)
XLA Ops:
  0.6 37.2 %shard_map.200.packed = f32[56,256]{1,0:T(8,128)S(1)} custom-call(f32[16,256,256]{2,1,0:T(8,128)} %refs_0_.1, f32[16,64,256]{2,1,0:T(8,128)} %refs_1_.1, f32[16,256,256]{2,1,0:T(8,128)} %refs_2_.1, f32[16,64,256]{2,1,0:T(8,128)} %refs_3_.1, f32[16,256,256]{2,1,0:T(8,128)} %refs_4_.1, f32[16,64,64]{2,1,0:T(8,128)} %refs_5_.1, f32[64,64]{1,0:T(8,128)} %refs_6_.1, ...), custom_call_target="tpu_custom_call" | custom-call | tf_op jit(solution)/shard_map/pallas_call | solution.py:556
  37.8 0.7 %shard_map.201 = (f32[16,256]{1,0:T(8,128)}, f32[16,64]{1,0:T(8,128)}, f32[16,256]{1,0:T(8,128)}, f32[16,64]{1,0:T(8,128)}, f32[1,3]{1,0:T(1,128)}) custom-call(f32[56,256]{1,0:T(8,128)S(1)} %shard_map.200.packed), custom_call_target="tpu_custom_call" | custom-call | tf_op jit(solution)/shard_map/pallas_call | solution.py:567

commit v3 on v2

--- a/solution.py
+++ b/solution.py
@@ -24,6 +24,16 @@
     ah, al = parts_of(a)
     bh, bl = parts_of(b)
     dot = functools.partial(jnp.dot, preferred_element_type=F32)
+    return dot(ah, bh) + (dot(ah, bl) + dot(al, bh))
+
+
+def matmul_nt(a, b):
+    ah, al = parts_of(a)
+    bh, bl = parts_of(b)
+
+    def dot(x, y):
+        return lax.dot_general(x, y, (((1,), (1,)), ((), ())), preferred_element_type=F32)
+
     return dot(ah, bh) + (dot(ah, bl) + dot(al, bh))
 
 
@@ -73,11 +83,12 @@
      packed_out,
      a, b, m, fb, v, gi, w, sw, sl, il, of, ub, st, inp, mu, bm, ac,
      pre, suf, group, heads, tails, turned_w, turned_r,
+     hess, slope, spread_u, spread_g, fb_t, fed_local, settled,
      sources, pushes, back_local, back, cols,
      fol_in, prd_in, prd_out, fol_out, vec_b, vec_f, direct_in, direct_out,
-     ch_b_in, ch_f_in, ch_b_out, ch_f_out,
+     ch_b_in, ch_f_in, ch_b_out, ch_f_out, skip_in, skip_w, skip_g, own_g,
      load_sem, m_sem, nb_send, nb_recv, p_send, p_recv, b_send, b_recv, f_send, f_recv,
-     d_send, d_recv, ch_send, ch_recv) = refs
+     d_send, d_recv, ch_send, ch_recv, r_send, r_recv) = refs
     me = lax.axis_index("tm")
     place = lax.rem(me, size)
     base = me - place
@@ -88,6 +99,10 @@
     half = sections // 2
     last = sections - 1
     first_group, top_group = at_group == 0, at_group == groups - 1
+    relayed = groups == 4
+    to_skip = jnp.logical_and(relayed, at_group == 1)
+    to_top = jnp.logical_and(relayed, at_group == 2)
+    skipped = jnp.logical_and(relayed, at_group == 3)
 
     early = [(st_hbm, st), (in_hbm, inp), (mu_hbm, mu),
              (a_hbm.at[last], a.at[last]), (b_hbm.at[last], b.at[last])]
@@ -122,6 +137,12 @@
             for j in range(size):
                 greet(start + j)
 
+    if relayed:
+        for has, peer in ((to_skip, me + 2 * size), (skipped, me - 2 * size)):
+            @pl.when(has)
+            def _():
+                greet(peer)
+
     def remote(src, dst, send, recv, peer):
         return pltpu.make_async_remote_copy(
             src_ref=src, dst_ref=dst, send_sem=send, recv_sem=recv,
@@ -159,6 +180,7 @@
         lines = grown
 
     peers = size - 1 + jnp.where(first_group, 0, size) + jnp.where(top_group, 0, size)
+    peers = peers + jnp.where(jnp.logical_or(to_skip, skipped), 1, 0)
     pl.semaphore_wait(barrier, peers)
     to_earlier = remote(fol_out, fol_in, nb_send.at[0], nb_recv.at[0], me - 1)
     to_later = remote(prd_out, prd_in, nb_send.at[1], nb_recv.at[1], me + 1)
@@ -310,6 +332,31 @@
             slot = source - base
             remote(buffer.at[slot], buffer.at[slot], send.at[j], recv.at[j], source).wait_recv()
 
+    for k in range(sections):
+        fb_t[k] = turned(fb[k])
+    sends_direct = jnp.logical_and(first_group, jnp.logical_not(top_group))
+
+    @pl.when(sends_direct)
+    def _():
+        spread_u[last * nu:] = b[last]
+        spread_g[last * nu:] = matmul(gi[last], b[last])
+        stride = 5 if last % 5 == 0 else 1
+
+        @pl.loop(0, last // stride)
+        def _(i):
+            for j in range(stride):
+                k = i * stride + j
+                u = matmul_nt(b[k], suf[k + 1])
+                rows = pl.ds(pl.multiple_of(k * nu, nu), nu)
+                spread_u[rows] = u
+                spread_g[rows] = matmul(gi[k], u)
+
+        step = ns if (sections * nu) % ns == 0 else nu
+        total_h = jnp.zeros((ns, ns), F32)
+        for q in range(0, sections * nu, step):
+            total_h = total_h + matmul(spread_u[q:q + step].T, spread_g[q:q + step])
+        hess[...] = -total_h
+
     arrive(vec_b, b_send, b_recv)
     if size == 4:
         piece(along, bottom, 1, along).wait_recv()
@@ -347,9 +394,56 @@
         tails[f] = group[size - 1] if e == 1 else matmul(tails[f + 1], group[f + 1])
     whole = matmul(group[size - 1], heads[size - 1]) if size > 1 else group[0]
     heads[size] = whole
+    turned_w[...] = whole.T
+    up_w = remote(turned_w, skip_w, r_send.at[1], r_recv.at[1], me + size)
+    up_g = remote(own_g, skip_g, r_send.at[2], r_recv.at[2], me + size)
+    up_skip = remote(ch_f_out, skip_in, r_send.at[0], r_recv.at[0], me + 2 * size)
+
+    @pl.when(to_top)
+    def _():
+        up_w.start()
 
     for k in range(1, last, 2):
         m[k] = m[k].T
+
+    def middle(incoming):
+        incoming_c = column_block(incoming)
+        for k in range(sections):
+            back[k:k + 1] = lift(suf[k], incoming_c) + back_local[k:k + 1]
+        after = jnp.concatenate([back[1:], incoming], axis=0)
+        acc = jnp.zeros((nu, LANES), F32)
+        for k in range(sections):
+            acc = jnp.where(lane_u == k, times(b[k], after[k:k + 1]), acc)
+        held = grad_input + turned(acc)[:sections]
+        acc = jnp.zeros((nu, LANES), F32)
+        for k in range(sections):
+            gain = -times(gi[k], held[k:k + 1])
+            acc = jnp.where(lane_u == k, gain, acc)
+            pushes[k:k + 1] = times_t(b[k], gain)
+        forward_gain = turned(acc)[:sections]
+        return held, forward_gain
+
+    def end_term():
+        acc = jnp.zeros((ns, ns), F32)
+        for k in range(sections):
+            drive = -defect[k:k + 1]
+            if k:
+                drive = drive + pushes[k - 1:k]
+            acc = acc + suf[k] * drive
+        return row_of(jnp.sum(acc, axis=1, keepdims=True)) + pushes[last:]
+
+    direct = [
+        remote(direct_out, direct_in.at[place], d_send.at[j], d_recv.at[place], base + size + j)
+        for j in range(size)
+    ]
+
+    @pl.when(sends_direct)
+    def _():
+        slope[...] = matmul(tails[place], hess[...])
+        middle(held_in)
+        ended = end_term()
+        settled[...] = packed(ended, row_of(times(tails[place], ended)))
+        hess[...] = matmul_nt(slope[...], tails[place])
 
     @pl.when(jnp.logical_not(top_group))
     def _():
@@ -363,51 +457,30 @@
         to_before.start()
 
     above = ch_b_in[1:2]
-    incoming = held_in + lift(tails[place], column_block(ch_b_in[0:1]))
-    incoming_c = column_block(incoming)
-    for k in range(sections):
-        back[k:k + 1] = lift(suf[k], incoming_c) + back_local[k:k + 1]
-    before = back[...]
-    after = jnp.concatenate([before[1:], incoming], axis=0)
-    acc = jnp.zeros((nu, LANES), F32)
-    for k in range(sections):
-        acc = jnp.where(lane_u == k, times(b[k], after[k:k + 1]), acc)
-    pulled = turned(acc)[:sections]
-    held = grad_input + pulled
-    acc = jnp.zeros((nu, LANES), F32)
-    for k in range(sections):
-        gain = -times(gi[k], held[k:k + 1])
-        acc = jnp.where(lane_u == k, gain, acc)
-        pushes[k:k + 1] = times_t(b[k], gain)
-    forward_gain = turned(acc)[:sections]
-
-    acc = jnp.zeros((ns, ns), F32)
-    for k in range(sections):
-        drive = -defect[k:k + 1]
-        if k:
-            drive = drive + pushes[k - 1:k]
-        acc = acc + suf[k] * drive
-    ended = row_of(jnp.sum(acc, axis=1, keepdims=True)) + pushes[last:]
-    vec_f[pl.ds(place, 1)] = ended[None]
+    coming_c = column_block(ch_b_in[0:1])
+
     f_copies = [
         remote(vec_f.at[place], vec_f.at[place], f_send.at[j], f_recv.at[j], mate)
         for j, mate in enumerate(mates)
     ]
-    direct = [
-        remote(direct_out, direct_in.at[place], d_send.at[j], d_recv.at[place], base + size + j)
-        for j in range(size)
-    ]
-    sends_direct = jnp.logical_and(first_group, jnp.logical_not(top_group))
 
     @pl.when(sends_direct)
     def _():
-        direct_out[...] = packed(row_of(times(tails[place], ended)), group_stats)
+        direct_out[...] = packed(settled[1:2] + lift(hess[...], coming_c), group_stats)
         for copy in direct:
             copy.start()
-
-    for copy in f_copies:
-        copy.start()
-    turned_w[...] = heads[size].T
+        vec_f[pl.ds(place, 1)] = (settled[0:1] + lift(slope[...], coming_c))[None]
+        for copy in f_copies:
+            copy.start()
+
+    held, forward_gain = middle(held_in + lift(tails[place], coming_c))
+
+    @pl.when(jnp.logical_not(sends_direct))
+    def _():
+        vec_f[pl.ds(place, 1)] = end_term()[None]
+        for copy in f_copies:
+            copy.start()
+
     turned_r[...] = heads[place].T
 
     drive = jnp.concatenate([jnp.zeros((1, ns), F32), pushes[:last]], axis=0) - defect
@@ -426,6 +499,14 @@
     kept.append(jnp.zeros((LANES - sections, ns), F32))
     cols[...] = acc + jnp.concatenate(kept, axis=0).T
 
+    moved = cols[:, :sections] - defect_t
+    acc = jnp.zeros((nu, LANES), F32)
+    alone = cols[...].T
+    for k in range(sections):
+        packed_out[sections + k:sections + k + 1] = times_t(v[k], moved[:, k:k + 1]) + back[k:k + 1]
+        acc = jnp.where(lane_u == k, times(fb[k], alone[k:k + 1]), acc)
+    fed_local[...] = turned(acc)[:sections]
+
     arrive(vec_f, f_send, f_recv)
     held_on = jnp.zeros((1, ns), F32)
     y = vec_f[0]
@@ -446,33 +527,53 @@
             came = came + direct_in[j, 0:1]
         ch_f_in[...] = packed(came, direct_in[0, 1:2])
 
-    @pl.when(at_group > 1)
+    @pl.when(to_top)
+    def _():
+        own_g[...] = packed(y, group_stats)
+        up_g.start()
+
+    @pl.when(jnp.logical_and(at_group > 1, jnp.logical_not(skipped)))
     def _():
         to_after.wait_recv()
+
+    @pl.when(skipped)
+    def _():
+        up_w.wait_recv()
+        up_g.wait_recv()
+        up_skip.wait_recv()
+        ch_f_in[...] = packed(
+            skip_g[0:1] + lift(skip_w[...], column_block(skip_in[0:1])), skip_g[1:2] + skip_in[1:2]
+        )
 
     below = ch_f_in[1:2]
     entering_c = column_block(ch_f_in[0:1])
-    goes_on = jnp.logical_and(jnp.logical_not(first_group), jnp.logical_not(top_group))
+    goes_on = jnp.logical_not(jnp.logical_or(jnp.logical_or(first_group, top_group), to_top))
 
     @pl.when(goes_on)
     def _():
         ch_f_out[...] = packed(y + lift(turned_w[...], entering_c), below + group_stats)
         to_after.start()
 
+    @pl.when(to_skip)
+    def _():
+        up_skip.start()
+
     entering = held_on + lift(turned_r[...], entering_c)
 
-    acc = cols[...] + jnp.where(lane == 0, column(entering), 0.0)
-    for k in range(1, sections):
-        acc = acc + jnp.where(lane == k, times(pre[k - 1], entering), 0.0)
-    state_step = acc.T[:sections]
-    packed_out[0:sections] = state_step
-    moved = acc[:, :sections] - defect_t
+    acc = cols[...]
+    fed = []
     for k in range(sections):
-        packed_out[sections + k:sections + k + 1] = times_t(v[k], moved[:, k:k + 1]) + back[k:k + 1]
-    acc = jnp.zeros((nu, LANES), F32)
-    for k in range(sections):
-        acc = jnp.where(lane_u == k, times(fb[k], state_step[k:k + 1]), acc)
-    fed = turned(acc)[:sections]
+        if k:
+            block = jnp.broadcast_to(times(pre[k - 1], entering), (ns, LANES))
+        else:
+            block = column_block(entering)
+        acc = acc + jnp.where(lane == k, block, 0.0)
+        packed_out[sections + k:sections + k + 1] = (
+            packed_out[sections + k:sections + k + 1] + lift(v[k], block)
+        )
+        fed.append(lift(fb_t[k], block))
+    packed_out[0:sections] = acc.T[:sections]
+    fed = jnp.concatenate(fed, axis=0) + fed_local[...]
     chosen = ac[...].astype(F32)
     input_step = (1.0 - chosen) * (fed + forward_gain) + chosen * (ub[...] - inp[...])
     bound_step = chosen * (
@@ -514,6 +615,15 @@
     def _():
         to_after.wait_send()
 
+    @pl.when(to_skip)
+    def _():
+        up_skip.wait_send()
+
+    @pl.when(to_top)
+    def _():
+        up_w.wait_send()
+        up_g.wait_send()
+
 
 def spread(sections, ns, nu, packed, o_state, o_input, o_mult, o_bound, o_norm):
     o_state[...] = packed[0:sections]
@@ -538,6 +648,13 @@
         pltpu.VMEM((size, ns, ns), F32),
         pltpu.VMEM((ns, ns), F32),
         pltpu.VMEM((ns, ns), F32),
+        pltpu.VMEM((ns, ns), F32),
+        pltpu.VMEM((ns, ns), F32),
+        pltpu.VMEM((sections * nu, ns), F32),
+        pltpu.VMEM((sections * nu, ns), F32),
+        pltpu.VMEM((sections, ns, nu), F32),
+        pltpu.VMEM((sections, nu), F32),
+        pltpu.VMEM((2, ns), F32),
         pltpu.VMEM((sections, ns), F32),
         pltpu.VMEM((sections, ns), F32),
         pltpu.VMEM((sections, ns), F32),
@@ -547,10 +664,11 @@
         pltpu.VMEM((size, 2, ns), F32),
         pltpu.VMEM((size, 1, ns), F32),
         pltpu.VMEM((size, 2, ns), F32),
-    ] + [pltpu.VMEM((2, ns), F32)] * 5 + [
+    ] + [pltpu.VMEM((2, ns), F32)] * 6 + [
+        pltpu.VMEM((ns, ns), F32), pltpu.VMEM((2, ns), F32), pltpu.VMEM((2, ns), F32),
         dma((18,)), dma((sections,)), dma((2,)), dma((2,)),
         dma((6,)), dma((6,)), dma((mates,)), dma((mates,)), dma((mates,)), dma((mates,)),
-        dma((size,)), dma((size,)), dma((2,)), dma((2,)),
+        dma((size,)), dma((size,)), dma((2,)), dma((2,)), dma((3,)), dma((3,)),
     ]
     args = [pltpu.with_memory_space_constraint(x, pltpu.HBM) for x in args]
     packed = pl.pallas_call(

time: 38.6 us -> 36 us (0.933)
  the two profiles are of different devices: /device:TPU:24 before, /device:TPU:0 now
where the time goes in v3:
time: 36 us; the launch traced here: 35.8 us
  Pallas kernels  35.2 us (98%)
  between operations  0.65 us (2%)
    pallas_call x1, Pallas kernels, local(): pl.pallas_call(functools.partial(kernel, n, size), out_shape=jax.ShapeDty...  34.5 us

profile of v3, /device:TPU:0, one launch (start us, length us, event | category | flops | bytes accessed | tf_op | source)
XLA Modules:
  0.0 35.8 jit_solution(12901567821979913676)
XLA Ops:
  0.6 34.5 %shard_map.200.packed = f32[56,256]{1,0:T(8,128)S(1)} custom-call(f32[16,256,256]{2,1,0:T(8,128)} %refs_0_.1, f32[16,64,256]{2,1,0:T(8,128)} %refs_1_.1, f32[16,256,256]{2,1,0:T(8,128)} %refs_2_.1, f32[16,64,256]{2,1,0:T(8,128)} %refs_3_.1, f32[16,256,256]{2,1,0:T(8,128)} %refs_4_.1, f32[16,64,64]{2,1,0:T(8,128)} %refs_5_.1, f32[64,64]{1,0:T(8,128)} %refs_6_.1, ...), custom_call_target="tpu_custom_call" | custom-call | tf_op jit(solution)/shard_map/pallas_call | solution.py:674
  35.1 0.7 %shard_map.201 = (f32[16,256]{1,0:T(8,128)}, f32[16,64]{1,0:T(8,128)}, f32[16,256]{1,0:T(8,128)}, f32[16,64]{1,0:T(8,128)}, f32[1,3]{1,0:T(1,128)}) custom-call(f32[56,256]{1,0:T(8,128)S(1)} %shard_map.200.packed), custom_call_target="tpu_custom_call" | custom-call | tf_op jit(solution)/shard_map/pallas_call | solution.py:685

commit v4 on v3

--- a/solution.py
+++ b/solution.py
@@ -77,7 +77,7 @@
     return jnp.concatenate(parts, axis=1) if len(parts) > 1 else parts[0]
 
 
-def kernel(n, size, *refs):
+def kernel(n, size, parts, *refs):
     (a_hbm, b_hbm, m_hbm, k_hbm, v_hbm, gi_hbm, w_hbm, sw_hbm, sl_hbm, il_hbm, of_hbm, ub_hbm,
      st_hbm, in_hbm, mu_hbm, bm_hbm, ac_hbm,
      packed_out,
@@ -87,8 +87,9 @@
      sources, pushes, back_local, back, cols,
      fol_in, prd_in, prd_out, fol_out, vec_b, vec_f, direct_in, direct_out,
      ch_b_in, ch_f_in, ch_b_out, ch_f_out, skip_in, skip_w, skip_g, own_g,
+     twin_in, twin_out, twin_y, twin_w,
      load_sem, m_sem, nb_send, nb_recv, p_send, p_recv, b_send, b_recv, f_send, f_recv,
-     d_send, d_recv, ch_send, ch_recv, r_send, r_recv) = refs
+     d_send, d_recv, ch_send, ch_recv, r_send, r_recv, t_send, t_recv) = refs
     me = lax.axis_index("tm")
     place = lax.rem(me, size)
     base = me - place
@@ -100,6 +101,12 @@
     last = sections - 1
     first_group, top_group = at_group == 0, at_group == groups - 1
     relayed = groups == 4
+    paired = parts == 2 and groups > 2
+    part = lax.axis_index("batch")
+    twin = 1 - part
+    serves = jnp.logical_and(paired, part == 1)
+    served = jnp.logical_and(paired, part == 0)
+    inner_group = jnp.logical_not(jnp.logical_or(first_group, top_group))
     to_skip = jnp.logical_and(relayed, at_group == 1)
     to_top = jnp.logical_and(relayed, at_group == 2)
     skipped = jnp.logical_and(relayed, at_group == 3)
@@ -143,10 +150,24 @@
             def _():
                 greet(peer)
 
-    def remote(src, dst, send, recv, peer):
+    def greet_twin(peer):
+        pl.semaphore_signal(
+            barrier, inc=1, device_id={"tm": peer, "batch": twin}, device_id_type=MESH
+        )
+
+    if paired:
+        greet_twin(me)
+        for has, peer in ((jnp.logical_not(first_group), me - size),
+                          (jnp.logical_not(top_group), me + size)):
+            @pl.when(has)
+            def _():
+                greet_twin(peer)
+
+    def remote(src, dst, send, recv, peer, other=None):
+        device = {"tm": peer} if other is None else {"tm": peer, "batch": other}
         return pltpu.make_async_remote_copy(
             src_ref=src, dst_ref=dst, send_sem=send, recv_sem=recv,
-            device_id={"tm": peer}, device_id_type=MESH,
+            device_id=device, device_id_type=MESH,
         )
 
     for load in loads[:len(early)]:
@@ -181,6 +202,8 @@
 
     peers = size - 1 + jnp.where(first_group, 0, size) + jnp.where(top_group, 0, size)
     peers = peers + jnp.where(jnp.logical_or(to_skip, skipped), 1, 0)
+    if paired:
+        peers = peers + 1 + jnp.where(first_group, 0, 1) + jnp.where(top_group, 0, 1)
     pl.semaphore_wait(barrier, peers)
     to_earlier = remote(fol_out, fol_in, nb_send.at[0], nb_recv.at[0], me - 1)
     to_later = remote(prd_out, prd_in, nb_send.at[1], nb_recv.at[1], me + 1)
@@ -340,7 +363,7 @@
     def _():
         spread_u[last * nu:] = b[last]
         spread_g[last * nu:] = matmul(gi[last], b[last])
-        stride = 5 if last % 5 == 0 else 1
+        stride = 15 if last % 15 == 0 else 1
 
         @pl.loop(0, last // stride)
         def _(i):
@@ -384,6 +407,22 @@
     def _():
         to_before.start()
 
+    enter_twin = remote(ch_b_out, twin_in, t_send.at[0], t_recv.at[0], me - size, twin)
+    give_y = remote(ch_f_out, twin_y, t_send.at[1], t_recv.at[1], me, twin)
+    give_w = remote(heads.at[size], twin_w, t_send.at[2], t_recv.at[2], me, twin)
+    pass_on = remote(twin_out, twin_in, t_send.at[0], t_recv.at[0], me - size)
+    hand_back = remote(twin_out, ch_b_in, t_send.at[3], ch_recv.at[0], me - size, twin)
+    gives = jnp.logical_and(served, inner_group)
+    if paired:
+        @pl.when(jnp.logical_and(served, top_group))
+        def _():
+            enter_twin.start()
+
+        @pl.when(gives)
+        def _():
+            ch_f_out[...] = packed(y, group_stats)
+            give_y.start()
+
     unit = (lax.broadcasted_iota(jnp.int32, (ns, ns), 0)
             == lax.broadcasted_iota(jnp.int32, (ns, ns), 1)).astype(F32)
     heads[0] = unit
@@ -392,12 +431,21 @@
         heads[e] = group[0] if e == 1 else matmul(group[e - 1], heads[e - 1])
         f = size - 1 - e
         tails[f] = group[size - 1] if e == 1 else matmul(tails[f + 1], group[f + 1])
-    whole = matmul(group[size - 1], heads[size - 1]) if size > 1 else group[0]
-    heads[size] = whole
-    turned_w[...] = whole.T
+
+    @pl.when(inner_group)
+    def _():
+        whole = matmul(group[size - 1], heads[size - 1]) if size > 1 else group[0]
+        heads[size] = whole
+        turned_w[...] = whole.T
+
     up_w = remote(turned_w, skip_w, r_send.at[1], r_recv.at[1], me + size)
     up_g = remote(own_g, skip_g, r_send.at[2], r_recv.at[2], me + size)
     up_skip = remote(ch_f_out, skip_in, r_send.at[0], r_recv.at[0], me + 2 * size)
+
+    if paired:
+        @pl.when(gives)
+        def _():
+            give_w.start()
 
     @pl.when(to_top)
     def _():
@@ -448,13 +496,39 @@
     @pl.when(jnp.logical_not(top_group))
     def _():
         to_before.wait_recv()
+
+    carries = inner_group
+    if paired:
+        carries = jnp.logical_and(inner_group, jnp.logical_not(served))
+
+    @pl.when(carries)
+    def _():
         ch_b_out[...] = packed(
             y + lift(heads[size], column_block(ch_b_in[0:1])), ch_b_in[1:2] + group_stats
         )
-
-    @pl.when(jnp.logical_not(jnp.logical_or(top_group, first_group)))
-    def _():
         to_before.start()
+
+    helps = jnp.logical_and(serves, inner_group)
+    hops_on = jnp.logical_and(helps, at_group > 1)
+    if paired:
+        @pl.when(helps)
+        def _():
+            give_y.wait_recv()
+            give_w.wait_recv()
+            enter_twin.wait_recv()
+            twin_out[...] = packed(
+                twin_y[0:1] + lift(twin_w[...], column_block(twin_in[0:1])),
+                twin_y[1:2] + twin_in[1:2],
+            )
+            hand_back.start()
+
+        @pl.when(hops_on)
+        def _():
+            pass_on.start()
+
+        @pl.when(gives)
+        def _():
+            give_y.wait_send()
 
     above = ch_b_in[1:2]
     coming_c = column_block(ch_b_in[0:1])
@@ -602,9 +676,26 @@
     for copy in p_copies + b_copies + f_copies:
         copy.wait_send()
 
-    @pl.when(jnp.logical_not(first_group))
+    @pl.when(jnp.logical_or(jnp.logical_and(top_group, jnp.logical_not(first_group)), carries))
     def _():
         to_before.wait_send()
+
+    if paired:
+        @pl.when(jnp.logical_and(served, top_group))
+        def _():
+            enter_twin.wait_send()
+
+        @pl.when(gives)
+        def _():
+            give_w.wait_send()
+
+        @pl.when(helps)
+        def _():
+            hand_back.wait_send()
+
+        @pl.when(hops_on)
+        def _():
+            pass_on.wait_send()
 
     @pl.when(sends_direct)
     def _():
@@ -633,7 +724,7 @@
     o_norm[...] = packed[3 * sections:3 * sections + 1, 0:3]
 
 
-def local(n, *args):
+def local(n, parts, *args):
     size = 4 if n % 4 == 0 else (2 if n % 2 == 0 else 1)
     sections, ns = args[12].shape
     nu = args[13].shape[1]
@@ -666,13 +757,15 @@
         pltpu.VMEM((size, 2, ns), F32),
     ] + [pltpu.VMEM((2, ns), F32)] * 6 + [
         pltpu.VMEM((ns, ns), F32), pltpu.VMEM((2, ns), F32), pltpu.VMEM((2, ns), F32),
+    ] + [pltpu.VMEM((2, ns), F32)] * 3 + [
+        pltpu.VMEM((ns, ns), F32),
         dma((18,)), dma((sections,)), dma((2,)), dma((2,)),
         dma((6,)), dma((6,)), dma((mates,)), dma((mates,)), dma((mates,)), dma((mates,)),
-        dma((size,)), dma((size,)), dma((2,)), dma((2,)), dma((3,)), dma((3,)),
+        dma((size,)), dma((size,)), dma((2,)), dma((2,)), dma((3,)), dma((3,)), dma((4,)), dma((3,)),
     ]
     args = [pltpu.with_memory_space_constraint(x, pltpu.HBM) for x in args]
     packed = pl.pallas_call(
-        functools.partial(kernel, n, size),
+        functools.partial(kernel, n, size, parts),
         out_shape=jax.ShapeDtypeStruct((3 * sections + 8, ns), F32),
         in_specs=[pl.BlockSpec(memory_space=pltpu.HBM)] * len(args),
         out_specs=pl.BlockSpec(memory_space=pltpu.VMEM),
@@ -698,6 +791,6 @@
     in_specs = (wide,) * 6 + (P("batch", None),) + (flat,) * 10
     out_specs = (flat,) * 4 + (P("batch"),)
     return jax.shard_map(
-        functools.partial(local, mesh.shape["tm"]),
+        functools.partial(local, mesh.shape["tm"], mesh.shape["batch"]),
         mesh=mesh, in_specs=in_specs, out_specs=out_specs, check_vma=False,
     )

time: 36 us -> 34.5 us (0.958)
  the two profiles are of different devices: /device:TPU:0 before, /device:TPU:24 now
where the time goes in v4:
time: 34.5 us; the launch traced here: 34.1 us
  Pallas kernels  33.4 us (97%)
  between operations  0.65 us (2%)
    pallas_call x1, Pallas kernels, local(): pl.pallas_call(functools.partial(kernel, n, size, parts), out_shape=jax.S...  32.7 us

profile of v4, /device:TPU:24, one launch (start us, length us, event | category | flops | bytes accessed | tf_op | source)
XLA Modules:
  0.0 34.1 jit_solution(17016191794513740364)
XLA Ops:
  0.6 32.7 %shard_map.200.packed = f32[56,256]{1,0:T(8,128)S(1)} custom-call(f32[16,256,256]{2,1,0:T(8,128)} %refs_0_.1, f32[16,64,256]{2,1,0:T(8,128)} %refs_1_.1, f32[16,256,256]{2,1,0:T(8,128)} %refs_2_.1, f32[16,64,256]{2,1,0:T(8,128)} %refs_3_.1, f32[16,256,256]{2,1,0:T(8,128)} %refs_4_.1, f32[16,64,64]{2,1,0:T(8,128)} %refs_5_.1, f32[64,64]{1,0:T(8,128)} %refs_6_.1, ...), custom_call_target="tpu_custom_call" | custom-call | tf_op jit(solution)/shard_map/pallas_call | solution.py:767
  33.4 0.7 %shard_map.201 = (f32[16,256]{1,0:T(8,128)}, f32[16,64]{1,0:T(8,128)}, f32[16,256]{1,0:T(8,128)}, f32[16,64]{1,0:T(8,128)}, f32[1,3]{1,0:T(1,128)}) custom-call(f32[56,256]{1,0:T(8,128)S(1)} %shard_map.200.packed), custom_call_target="tpu_custom_call" | custom-call | tf_op jit(solution)/shard_map/pallas_call | solution.py:778

commit v5 on v4

--- a/solution.py
+++ b/solution.py
@@ -87,7 +87,7 @@
      sources, pushes, back_local, back, cols,
      fol_in, prd_in, prd_out, fol_out, vec_b, vec_f, direct_in, direct_out,
      ch_b_in, ch_f_in, ch_b_out, ch_f_out, skip_in, skip_w, skip_g, own_g,
-     twin_in, twin_out, twin_y, twin_w,
+     twin_in, twin_out, twin_y, twin_w, joins,
      load_sem, m_sem, nb_send, nb_recv, p_send, p_recv, b_send, b_recv, f_send, f_recv,
      d_send, d_recv, ch_send, ch_recv, r_send, r_recv, t_send, t_recv) = refs
     me = lax.axis_index("tm")
@@ -355,8 +355,11 @@
             slot = source - base
             remote(buffer.at[slot], buffer.at[slot], send.at[j], recv.at[j], source).wait_recv()
 
-    for k in range(sections):
-        fb_t[k] = turned(fb[k])
+    @pl.when(jnp.logical_not(first_group))
+    def _():
+        for k in range(sections):
+            fb_t[k] = turned(fb[k])
+
     sends_direct = jnp.logical_and(first_group, jnp.logical_not(top_group))
 
     @pl.when(sends_direct)
@@ -427,25 +430,35 @@
             == lax.broadcasted_iota(jnp.int32, (ns, ns), 1)).astype(F32)
     heads[0] = unit
     tails[size - 1] = unit
-    for e in range(1, size):
+
+    def widen(e):
         heads[e] = group[0] if e == 1 else matmul(group[e - 1], heads[e - 1])
         f = size - 1 - e
         tails[f] = group[size - 1] if e == 1 else matmul(tails[f + 1], group[f + 1])
 
+    middle_e = size // 2
+    for e in range(1, middle_e + 1):
+        widen(e)
+
     @pl.when(inner_group)
     def _():
-        whole = matmul(group[size - 1], heads[size - 1]) if size > 1 else group[0]
-        heads[size] = whole
-        turned_w[...] = whole.T
+        heads[size] = matmul(tails[middle_e - 1], heads[middle_e]) if size > 1 else group[0]
+
+    if paired:
+        @pl.when(gives)
+        def _():
+            give_w.start()
+
+    for e in range(middle_e + 1, size):
+        widen(e)
+
+    @pl.when(inner_group)
+    def _():
+        turned_w[...] = heads[size].T
 
     up_w = remote(turned_w, skip_w, r_send.at[1], r_recv.at[1], me + size)
     up_g = remote(own_g, skip_g, r_send.at[2], r_recv.at[2], me + size)
     up_skip = remote(ch_f_out, skip_in, r_send.at[0], r_recv.at[0], me + 2 * size)
-
-    if paired:
-        @pl.when(gives)
-        def _():
-            give_w.start()
 
     @pl.when(to_top)
     def _():
@@ -557,6 +570,12 @@
 
     turned_r[...] = heads[place].T
 
+    @pl.when(jnp.logical_and(first_group, me > 0))
+    def _():
+        for k in range(sections):
+            fb_t[k] = turned(fb[k])
+
+
     drive = jnp.concatenate([jnp.zeros((1, ns), F32), pushes[:last]], axis=0) - defect
     drive_t = turned(drive)
     step = drive[0:1]
@@ -581,12 +600,21 @@
         acc = jnp.where(lane_u == k, times(fb[k], alone[k:k + 1]), acc)
     fed_local[...] = turned(acc)[:sections]
 
-    arrive(vec_f, f_send, f_recv)
-    held_on = jnp.zeros((1, ns), F32)
-    y = vec_f[0]
-    for e in range(1, size):
-        held_on = jnp.where(place == e, y, held_on)
-        y = vec_f[e] + row_of(times(group[e], y))
+    starts = me == 0
+
+    @pl.when(jnp.logical_not(starts))
+    def _():
+        arrive(vec_f, f_send, f_recv)
+        held_on = jnp.zeros((1, ns), F32)
+        y = vec_f[0]
+        for e in range(1, size):
+            held_on = jnp.where(place == e, y, held_on)
+            y = vec_f[e] + row_of(times(group[e], y))
+        joins[...] = packed(y, held_on)
+
+    @pl.when(starts)
+    def _():
+        joins[...] = jnp.zeros_like(joins)
 
     @pl.when(first_group)
     def _():
@@ -603,7 +631,7 @@
 
     @pl.when(to_top)
     def _():
-        own_g[...] = packed(y, group_stats)
+        own_g[...] = packed(joins[0:1], group_stats)
         up_g.start()
 
     @pl.when(jnp.logical_and(at_group > 1, jnp.logical_not(skipped)))
@@ -625,29 +653,37 @@
 
     @pl.when(goes_on)
     def _():
-        ch_f_out[...] = packed(y + lift(turned_w[...], entering_c), below + group_stats)
+        ch_f_out[...] = packed(joins[0:1] + lift(turned_w[...], entering_c), below + group_stats)
         to_after.start()
 
     @pl.when(to_skip)
     def _():
         up_skip.start()
 
-    entering = held_on + lift(turned_r[...], entering_c)
-
-    acc = cols[...]
-    fed = []
-    for k in range(sections):
-        if k:
-            block = jnp.broadcast_to(times(pre[k - 1], entering), (ns, LANES))
-        else:
-            block = column_block(entering)
-        acc = acc + jnp.where(lane == k, block, 0.0)
-        packed_out[sections + k:sections + k + 1] = (
-            packed_out[sections + k:sections + k + 1] + lift(v[k], block)
-        )
-        fed.append(lift(fb_t[k], block))
-    packed_out[0:sections] = acc.T[:sections]
-    fed = jnp.concatenate(fed, axis=0) + fed_local[...]
+    entering = joins[1:2] + lift(turned_r[...], entering_c)
+
+    @pl.when(starts)
+    def _():
+        packed_out[0:sections] = cols[...].T[:sections]
+
+    @pl.when(jnp.logical_not(starts))
+    def _():
+        acc = jnp.zeros((ns, LANES), F32)
+        fed = []
+        for k in range(sections):
+            if k:
+                block = jnp.broadcast_to(times(pre[k - 1], entering), (ns, LANES))
+            else:
+                block = column_block(entering)
+            acc = jnp.where(lane == k, block, acc)
+            packed_out[sections + k:sections + k + 1] = (
+                packed_out[sections + k:sections + k + 1] + lift(v[k], block)
+            )
+            fed.append(lift(fb_t[k], block))
+        packed_out[0:sections] = (cols[...] + acc).T[:sections]
+        fed_local[...] = fed_local[...] + jnp.concatenate(fed, axis=0)
+
+    fed = fed_local[...]
     chosen = ac[...].astype(F32)
     input_step = (1.0 - chosen) * (fed + forward_gain) + chosen * (ub[...] - inp[...])
     bound_step = chosen * (
@@ -664,6 +700,10 @@
     entries = jnp.where(spot == 0, ns, jnp.where(spot == 1, ns + nu, nu)).astype(F32)
     norms = jnp.sqrt(tops / (scale + floor_share * horizon * entries))
     packed_out[3 * sections:3 * sections + 1, 0:3] = norms
+
+    @pl.when(starts)
+    def _():
+        arrive(vec_f, f_send, f_recv)
 
     @pl.when(me > 0)
     def _():
@@ -758,7 +798,7 @@
     ] + [pltpu.VMEM((2, ns), F32)] * 6 + [
         pltpu.VMEM((ns, ns), F32), pltpu.VMEM((2, ns), F32), pltpu.VMEM((2, ns), F32),
     ] + [pltpu.VMEM((2, ns), F32)] * 3 + [
-        pltpu.VMEM((ns, ns), F32),
+        pltpu.VMEM((ns, ns), F32), pltpu.VMEM((2, ns), F32),
         dma((18,)), dma((sections,)), dma((2,)), dma((2,)),
         dma((6,)), dma((6,)), dma((mates,)), dma((mates,)), dma((mates,)), dma((mates,)),
         dma((size,)), dma((size,)), dma((2,)), dma((2,)), dma((3,)), dma((3,)), dma((4,)), dma((3,)),

time: 34.5 us -> 33.8 us (0.980)
  Pallas kernels: 33.4 us -> 33 us
    pallas_call x1, Pallas kernels: 32.7 us -> 32.3 us  [local(): pl.pallas_call(functools.partial(kernel, n, size, parts), out_shape=jax.S...]
where the time goes in v5:
time: 33.8 us; the launch traced here: 33.6 us
  Pallas kernels  33 us (98%)
  between operations  0.65 us (2%)
    pallas_call x1, Pallas kernels, local(): pl.pallas_call(functools.partial(kernel, n, size, parts), out_shape=jax.S...  32.3 us

profile of v5, /device:TPU:24, one launch (start us, length us, event | category | flops | bytes accessed | tf_op | source)
XLA Modules:
  0.0 33.6 jit_solution(5463720183656821042)
XLA Ops:
  0.6 32.3 %shard_map.200.packed = f32[56,256]{1,0:T(8,128)S(1)} custom-call(f32[16,256,256]{2,1,0:T(8,128)} %refs_0_.1, f32[16,64,256]{2,1,0:T(8,128)} %refs_1_.1, f32[16,256,256]{2,1,0:T(8,128)} %refs_2_.1, f32[16,64,256]{2,1,0:T(8,128)} %refs_3_.1, f32[16,256,256]{2,1,0:T(8,128)} %refs_4_.1, f32[16,64,64]{2,1,0:T(8,128)} %refs_5_.1, f32[64,64]{1,0:T(8,128)} %refs_6_.1, ...), custom_call_target="tpu_custom_call" | custom-call | tf_op jit(solution)/shard_map/pallas_call | solution.py:807
  32.9 0.7 %shard_map.201 = (f32[16,256]{1,0:T(8,128)}, f32[16,64]{1,0:T(8,128)}, f32[16,256]{1,0:T(8,128)}, f32[16,64]{1,0:T(8,128)}, f32[1,3]{1,0:T(1,128)}) custom-call(f32[56,256]{1,0:T(8,128)S(1)} %shard_map.200.packed), custom_call_target="tpu_custom_call" | custom-call | tf_op jit(solution)/shard_map/pallas_call | solution.py:818
